TPU v7x, 32 devices: a whole 2x2x4 slice. The times are simulated.
32 devices in a mesh: samples: 4 (over y, x), features: 4 (over z), rhs: 2 (over core).
Axes of the slice: x: 2, y: 2, z: 4, core: 2. Of those that a mesh axis runs over, the one named last changes fastest.
Arguments:
- design: bfloat16 [32768, 32768], P(('samples', 'rhs'), 'features'), may hold values from -0.03125 to 0.03125
- right_side: float32 [32768, 64], P('features', 'rhs'), may hold values from -6 to 6
- factor: bfloat16 [32768, 768], P('features', 'rhs'), may hold values from -0.03125 to 0.03125
- nystrom_values: float32 [768], replicated, may hold values from 0.5 to 3
Outputs:
- solution: float32 [32768, 64], P('features', 'rhs')
- residual: float32 [32768, 64], P('features', 'rhs')
All inputs are finite; a program needn't handle non-finite values.
Results may differ from a plain program's by a relative error of at most 0.0181.
Values may be sent and summed in bfloat16 or wider, within the bound.
A program may use at most 192 MiB of HBM per device.

v0:
```python
import jax
import jax.numpy as jnp
from jax import lax
from jax.sharding import PartitionSpec as P

ITERS = 3
ridge_weight = 1.0


def inner_prod(left, right):
    return lax.dot_general(
        left,
        right,
        (((0,), (0,)), ((), ())),
        precision=lax.Precision.HIGHEST,
        preferred_element_type=jnp.float32,
    )


def split_parts(values):
    upper = values.astype(jnp.bfloat16)
    widened = lax.optimization_barrier(upper).astype(jnp.float32)
    lower = (values - widened).astype(jnp.bfloat16)
    return (upper, lower)


def factor_inner(factor_narrow, values):
    upper, lower = split_parts(values)
    dims = (((0,), (0,)), ((), ()))
    first = lax.dot_general(factor_narrow, upper, dims, preferred_element_type=jnp.float32)
    second = lax.dot_general(factor_narrow, lower, dims, preferred_element_type=jnp.float32)
    return first + second


def factor_times(factor_narrow, values):
    upper, lower = split_parts(values)
    first = jnp.dot(factor_narrow, upper, preferred_element_type=jnp.float32)
    second = jnp.dot(factor_narrow, lower, preferred_element_type=jnp.float32)
    return first + second


def shards(design, right_side, factor, nystrom_values):
    feat_rows, col_share = right_side.shape
    shrink = (1.0 + jnp.min(nystrom_values)) / (1.0 + nystrom_values) - 1.0
    columns = lax.all_gather(right_side, "rhs", axis=1, tiled=True)
    residual = columns
    basis_rows = lax.all_gather(factor, "rhs", axis=1, tiled=True)

    def totals(values):
        return lax.psum(values, "features")

    def expand(projected):
        return factor_times(basis_rows, shrink[:, None] * projected)

    projected = totals(factor_inner(basis_rows, residual))
    direction = residual + expand(projected)
    solution = jnp.zeros_like(residual)
    for iteration in range(ITERS):
        narrow = direction.astype(jnp.bfloat16)
        apply_partial_value = jnp.dot(design, narrow, preferred_element_type=jnp.float32)
        narrow_images = lax.psum(apply_partial_value, "features").astype(jnp.bfloat16)
        feature_term = lax.dot_general(
            design, narrow_images, (((0,), (0,)), ((), ())), preferred_element_type=jnp.float32
        )
        summed = lax.psum(feature_term, ("samples", "rhs"))
        applied = summed + ridge_weight * direction
        gram_block, cross_term, image_res, image_image, factor_image = totals(
            (
                inner_prod(direction, applied),
                inner_prod(direction, residual),
                inner_prod(applied, residual),
                inner_prod(applied, applied),
                factor_inner(basis_rows, applied),
            )
        )
        gram_block = 0.5 * (gram_block + gram_block.T)
        chol_lower = jnp.linalg.cholesky(gram_block)
        unit_dir = jax.scipy.linalg.solve_triangular(chol_lower, direction.T, lower=True).T
        unit_img = jax.scipy.linalg.solve_triangular(chol_lower, applied.T, lower=True).T
        step_coef = jax.scipy.linalg.solve_triangular(chol_lower, cross_term, lower=True)
        solution = solution + jnp.dot(unit_dir, step_coef, precision=lax.Precision.HIGHEST)
        residual = residual - jnp.dot(unit_img, step_coef, precision=lax.Precision.HIGHEST)
        if iteration + 1 < ITERS:
            back_step = jax.scipy.linalg.solve_triangular(
                chol_lower, step_coef, lower=True, trans=1
            )
            projected = projected - jnp.dot(
                factor_image, back_step, precision=lax.Precision.HIGHEST
            )
            scaled = residual + expand(projected)
            image_new = image_res - jnp.dot(image_image, back_step, precision=lax.Precision.HIGHEST)
            image_new = image_new + inner_prod(factor_image, shrink[:, None] * projected)
            next_coef = -jax.scipy.linalg.solve_triangular(chol_lower, image_new, lower=True)
            direction = scaled + jnp.dot(unit_dir, next_coef, precision=lax.Precision.HIGHEST)
    column_start = lax.axis_index("rhs") * col_share
    out_sol = lax.dynamic_slice_in_dim(solution, column_start, col_share, 1)
    out_res = lax.dynamic_slice_in_dim(residual, column_start, col_share, 1)
    return (out_sol, out_res)


def solution(mesh):
    placed = (P(("samples", "rhs"), "features"), P("features", "rhs"), P("features", "rhs"), P())
    return jax.shard_map(
        shards,
        mesh=mesh,
        in_specs=placed,
        out_specs=(P("features", "rhs"), P("features", "rhs")),
        check_vma=False,
    )
```

profile of v0, /device:TPU:0, one launch (start us, length us, event | category | flops | bytes accessed | tf_op | source)
XLA Modules:
  0.0 853.2 jit_solution(9998928612973178029)
XLA Ops:
  10.0 12.9 %all-gather.3.cloned.1.call-done = f32[8192,64]{0,1:T(8,128)} async-done(((f32[8192,32]{0,1:T(8,128)}), f32[8192,64]{0,1:T(8,128)}) %all-gather.3.cloned.1.call-update) | async-done | bytes 2097168 | tf_op jit(solution)/shard_map/all_gather | solution.py:45
  24.7 25.6 %all-gather.5.cloned.1.call-done = bf16[8192,768]{1,0:T(8,128)(2,1)} async-done(((bf16[8192,384]{1,0:T(8,128)(2,1)}), bf16[8192,768]{1,0:T(8,128)(2,1)}) %all-gather.5.cloned.1.call-update) | async-done | bytes 12582928 | tf_op jit(solution)/shard_map/all_gather | solution.py:47
  50.3 7.0 convolution_bitcast_fusion.6
  61.5 36.2 %all-reduce.15.cloned.1.call-done = f32[768,64]{0,1:T(8,128)} async-done(((f32[768,64]{0,1:T(8,128)}), f32[768,64]{0,1:T(8,128)}) %all-reduce.15.cloned.1.call-update) | async-done | bytes 196624 | tf_op jit(solution)/shard_map/psum | solution.py:50
  98.7 8.5 fusion.67
  107.2 9.8 %fusion.3 = f32[8192,64]{0,1:T(8,128)} fusion(f32[8192,64]{0,1:T(8,128)S(1)} %copy-done.1, f32[64,8192]{1,0:T(8,128)S(1)} %fusion.67, bf16[8192,768]{1,0:T(8,128)(2,1)} %all-gather.5.cloned.1.call-done, bf16[768,64]{0,1:T(8,128)(2,1)S(1)} %multiply_convert_fusion, f32[768,64]{0,1:T(8,128)S(1)} %copy-done.19, f32[768]{0:T(1024)S(1)} %divide_add_fusion), kind=kOutput, calls=%fused_computation.13 | convolution fusion | flops 806551552 | bytes 19172352 | tf_op jit(solution)/shard_map/dot_general | solution.py:38
  117.1 30.4 %convolution_bitcast_fusion.5 = f32[4096,64]{0,1:T(8,128)S(1)} fusion(bf16[4096,8192]{1,0:T(8,128)(2,1)} %param.11, f32[8192,64]{0,1:T(8,128)} %fusion.3), kind=kOutput, calls=%fused_computation.18 | convolution fusion | flops 4295491584 | bytes 70254592 | tf_op jit(solution)/shard_map/dot_general | solution.py:60
  147.4 42.8 %all-reduce.30 = bf16[4096,64]{0,1:T(8,128)(2,1)} all-reduce(f32[4096,64]{0,1:T(8,128)S(1)} %convolution_bitcast_fusion.5), channel_id=1, replica_groups=mesh['samples'=4,'features'=4,'rhs'=2] {'features'}, use_global_device_ids=true, to_apply=%region_2.0 | all-reduce | flops 262144 | bytes 1572864 | tf_op jit(solution)/shard_map/psum | solution.py:61
  190.2 25.9 %convolution_bitcast_fusion.2 = f32[8192,64]{0,1:T(8,128)} fusion(bf16[4096,8192]{1,0:T(8,128)(2,1)} %param.11, bf16[4096,64]{0,1:T(8,128)(2,1)} %all-reduce.30), kind=kOutput, calls=%fused_computation.10 | convolution fusion | flops 4294967296 | bytes 69730304 | tf_op jit(solution)/shard_map/dot_general | solution.py:62
  220.2 57.3 %all-reduce.17.cloned.1.call-done = f32[8192,64]{0,1:T(8,128)} async-done(((f32[8192,64]{0,1:T(8,128)}), f32[8192,64]{0,1:T(8,128)}) %all-reduce.17.cloned.1.call-update) | async-done | bytes 2097168 | tf_op jit(solution)/shard_map/psum | solution.py:65
  287.3 6.8 fusion.71
  294.2 7.6 fusion.22
  302.0 19.4 %all-reduce.29.cloned.1.call-done = (f32[64,64]{1,0:T(8,128)}, f32[64,64]{1,0:T(8,128)}, f32[64,64]{1,0:T(8,128)}, f32[64,64]{1,0:T(8,128)}) async-done(((f32[64,64]{1,0:T(8,128)}, f32[64,64]{1,0:T(8,128)}, f32[64,64]{1,0:T(8,128)}, f32[64,64]{1,0:T(8,128)}), (f32[64,64]{1,0:T(8,128)}, f32[64,64]{1,0:T(8,128)}, f32[64,64]{1,0:T(8,128)}, f32[64,64]{1,0:T(8,128)})) %all-reduce.29.cloned.1.call-update) | async-done | bytes 65552 | tf_op jit(solution)/shard_map/psum | solution.py:50
  344.5 14.6 %all-reduce.19.cloned.1.call-done = f32[768,64]{0,1:T(8,128)} async-done(((f32[768,64]{0,1:T(8,128)}), f32[768,64]{0,1:T(8,128)}) %all-reduce.19.cloned.1.call-update) | async-done | bytes 196624 | tf_op jit(solution)/shard_map/psum | solution.py:50
  362.1 8.4 fusion.72
  370.6 8.6 %fusion.4 = f32[8192,64]{0,1:T(8,128)S(1)} fusion(f32[8192,64]{0,1:T(8,128)S(1)} %convolution_subtract_fusion.1, f32[64,8192]{1,0:T(8,128)S(1)} %fusion.72, bf16[8192,768]{1,0:T(8,128)(2,1)} %all-gather.5.cloned.1.call-done, bf16[768,64]{0,1:T(8,128)(2,1)S(1)} %get-tuple-element.20, f32[768,64]{0,1:T(8,128)S(1)} %get-tuple-element.21, ...), kind=kOutput, calls=%fused_computation.14 | convolution fusion | flops 806551552 | bytes 19172352 | tf_op jit(solution)/shard_map/dot_general | solution.py:38
  381.5 27.8 %convolution_bitcast_fusion.4 = f32[4096,64]{0,1:T(8,128)S(1)} fusion(bf16[4096,8192]{1,0:T(8,128)(2,1)} %param.11, f32[8192,64]{0,1:T(8,128)S(1)} %convolution_add_fusion.2), kind=kOutput, calls=%fused_computation.17 | convolution fusion | flops 4295491584 | bytes 70254592 | tf_op jit(solution)/shard_map/dot_general | solution.py:60
  409.4 42.1 %all-reduce.31 = bf16[4096,64]{0,1:T(8,128)(2,1)} all-reduce(f32[4096,64]{0,1:T(8,128)S(1)} %convolution_bitcast_fusion.4), channel_id=1, replica_groups=mesh['samples'=4,'features'=4,'rhs'=2] {'features'}, use_global_device_ids=true, to_apply=%region_11.0 | all-reduce | flops 262144 | bytes 1572864 | tf_op jit(solution)/shard_map/psum | solution.py:61
  451.5 25.9 %convolution_bitcast_fusion.1 = f32[8192,64]{0,1:T(8,128)} fusion(bf16[4096,8192]{1,0:T(8,128)(2,1)} %param.11, bf16[4096,64]{0,1:T(8,128)(2,1)} %all-reduce.31), kind=kOutput, calls=%fused_computation.5 | convolution fusion | flops 4294967296 | bytes 69730304 | tf_op jit(solution)/shard_map/dot_general | solution.py:62
  481.9 57.4 %all-reduce.21.cloned.1.call-done = f32[8192,64]{0,1:T(8,128)} async-done(((f32[8192,64]{0,1:T(8,128)}), f32[8192,64]{0,1:T(8,128)}) %all-reduce.21.cloned.1.call-update) | async-done | bytes 2097168 | tf_op jit(solution)/shard_map/psum | solution.py:65
  549.5 6.8 fusion.78
  556.4 7.6 fusion.23
  564.2 19.4 %all-reduce.27.cloned.1.call-done = (f32[64,64]{1,0:T(8,128)}, f32[64,64]{1,0:T(8,128)}, f32[64,64]{1,0:T(8,128)}, f32[64,64]{1,0:T(8,128)}) async-done(((f32[64,64]{1,0:T(8,128)}, f32[64,64]{1,0:T(8,128)}, f32[64,64]{1,0:T(8,128)}, f32[64,64]{1,0:T(8,128)}), (f32[64,64]{1,0:T(8,128)}, f32[64,64]{1,0:T(8,128)}, f32[64,64]{1,0:T(8,128)}, f32[64,64]{1,0:T(8,128)})) %all-reduce.27.cloned.1.call-update) | async-done | bytes 65552 | tf_op jit(solution)/shard_map/psum | solution.py:50
  585.3 5.8 cholesky.70
  606.6 14.8 %all-reduce.23.cloned.1.call-done = f32[768,64]{0,1:T(8,128)} async-done(((f32[768,64]{0,1:T(8,128)}), f32[768,64]{0,1:T(8,128)}) %all-reduce.23.cloned.1.call-update) | async-done | bytes 196624 | tf_op jit(solution)/shard_map/psum | solution.py:50
  624.5 8.4 fusion.79
  632.9 8.6 %fusion.5 = f32[8192,64]{0,1:T(8,128)S(1)} fusion(f32[8192,64]{0,1:T(8,128)S(1)} %convolution_subtract_fusion, f32[64,8192]{1,0:T(8,128)S(1)} %fusion.79, bf16[8192,768]{1,0:T(8,128)(2,1)} %all-gather.5.cloned.1.call-done, f32[768,64]{0,1:T(8,128)S(1)} %get-tuple-element.23, bf16[768,64]{0,1:T(8,128)(2,1)S(1)} %get-tuple-element.22), kind=kOutput, calls=%fused_computation.15 | convolution fusion | flops 806502400 | bytes 19169280 | tf_op jit(solution)/shard_map/dot_general | solution.py:38
  644.0 27.1 %convolution_bitcast_fusion.3 = f32[4096,64]{0,1:T(8,128)S(1)} fusion(bf16[4096,8192]{1,0:T(8,128)(2,1)} %param.11, f32[8192,64]{0,1:T(8,128)S(1)} %convolution_add_fusion), kind=kOutput, calls=%fused_computation.16 | convolution fusion | flops 4295491584 | bytes 70254592 | tf_op jit(solution)/shard_map/dot_general | solution.py:60
  671.1 42.1 %all-reduce.32 = bf16[4096,64]{0,1:T(8,128)(2,1)} all-reduce(f32[4096,64]{0,1:T(8,128)S(1)} %convolution_bitcast_fusion.3), channel_id=1, replica_groups=mesh['samples'=4,'features'=4,'rhs'=2] {'features'}, use_global_device_ids=true, to_apply=%region_18.0 | all-reduce | flops 262144 | bytes 1572864 | tf_op jit(solution)/shard_map/psum | solution.py:61
  713.2 25.9 %convolution_bitcast_fusion = f32[8192,64]{0,1:T(8,128)} fusion(bf16[4096,8192]{1,0:T(8,128)(2,1)} %param.11, bf16[4096,64]{0,1:T(8,128)(2,1)} %all-reduce.32), kind=kOutput, calls=%fused_computation | convolution fusion | flops 4294967296 | bytes 69730304 | tf_op jit(solution)/shard_map/dot_general | solution.py:62
  750.0 50.6 %all-reduce.25.cloned.1.call-done = f32[8192,64]{0,1:T(8,128)} async-done(((f32[8192,64]{0,1:T(8,128)}), f32[8192,64]{0,1:T(8,128)}) %all-reduce.25.cloned.1.call-update) | async-done | bytes 2097168 | tf_op jit(solution)/shard_map/psum | solution.py:65
  804.1 19.8 %all-reduce = (f32[64,64]{1,0:T(8,128)S(1)}, f32[64,64]{1,0:T(8,128)S(1)}) all-reduce(f32[64,64]{1,0:T(8,128)S(1)} %fusion.19, f32[64,64]{1,0:T(8,128)S(1)} %fusion.83), channel_id=1, replica_groups=mesh['samples'=4,'features'=4,'rhs'=2] {'features'}, use_global_device_ids=true, to_apply=%region_20.25 | all-reduce | flops 8192 | bytes 65536 | tf_op jit(solution)/shard_map/psum | solution.py:50
  (149 shorter events, 125.3 us)
Async XLA Ops:
  7.2 15.7 %all-gather.3.cloned.1.call-start = ((), (), s32[]{:S(2)}) async-start(), calls=%async_computation | async-start | bytes 3145728 | tf_op jit(solution)/shard_map/all_gather | solution.py:45
  7.9 42.4 %all-gather.5.cloned.1.call-start = ((), (), s32[]{:S(2)}) async-start(), calls=%async_computation.1 | async-start | bytes 18874368 | tf_op jit(solution)/shard_map/all_gather | solution.py:47
  8.7 89.1 %all-reduce.15.cloned.1.call-start = ((), (), s32[]{:S(2)}) async-start(), calls=%async_computation.2 | async-start | bytes 393216 | tf_op jit(solution)/shard_map/psum | solution.py:50
  22.8 27.4 %copy-start.1 = (f32[8192,64]{0,1:T(8,128)S(1)}, f32[8192,64]{0,1:T(8,128)}, u32[]{:S(2)}) copy-start(f32[8192,64]{0,1:T(8,128)} %all-gather.3.cloned.1.call-done) | copy-start | bytes 6291460
  50.3 8.2 copy-start
  61.5 216.0 %all-reduce.17.cloned.1.call-start = ((), (), s32[]{:S(2)}) async-start(), calls=%async_computation.3 | async-start | bytes 4194304 | tf_op jit(solution)/shard_map/psum | solution.py:65
  98.7 8.5 copy-start.19
  216.2 105.3 %all-reduce.29.cloned.1.call-start = ((), (), s32[]{:S(2)}) async-start(), calls=%async_computation.9 | async-start | bytes 262144 | tf_op jit(solution)/shard_map/psum | solution.py:50
  280.0 2.4 copy-start.4
  282.4 2.4 copy-start.2
  287.3 71.8 %all-reduce.19.cloned.1.call-start = ((), (), s32[]{:S(2)}) async-start(), calls=%async_computation.4 | async-start | bytes 393216 | tf_op jit(solution)/shard_map/psum | solution.py:50
  301.8 237.5 %all-reduce.21.cloned.1.call-start = ((), (), s32[]{:S(2)}) async-start(), calls=%async_computation.5 | async-start | bytes 4194304 | tf_op jit(solution)/shard_map/psum | solution.py:65
  340.0 2.2 copy-start.3
  342.2 19.4 %copy-start.24 = (f32[64,64]{1,0:T(8,128)S(1)}, f32[64,64]{1,0:T(8,128)}, u32[]{:S(2)}) copy-start(f32[64,64]{1,0:T(8,128)} %get-tuple-element.14) | copy-start | bytes 49156
  342.2 19.4 %copy-start.25 = (f32[64,64]{1,0:T(8,128)S(1)}, f32[64,64]{1,0:T(8,128)}, u32[]{:S(2)}) copy-start(f32[64,64]{1,0:T(8,128)} %get-tuple-element.15) | copy-start | bytes 49156
  344.3 26.2 %copy-start.7 = (f32[8192,64]{0,1:T(8,128)}, f32[8192,64]{0,1:T(8,128)S(1)}, u32[]{:S(2)}) copy-start(f32[8192,64]{0,1:T(8,128)S(1)} %convolution_subtract_fusion.1) | copy-start | bytes 6291460
  370.5 8.7 %copy-start.13 = (f32[64,8192]{1,0:T(8,128)S(1)}, f32[64,8192]{1,0:T(8,128)}, u32[]{:S(2)}) copy-start(f32[64,8192]{1,0:T(8,128)} %fusion.16) | copy-start | bytes 6291460
  381.5 96.4 %copy-start.5 = (f32[8192,64]{0,1:T(8,128)}, f32[8192,64]{0,1:T(8,128)S(1)}, u32[]{:S(2)}) copy-start(f32[8192,64]{0,1:T(8,128)S(1)} %convolution_add_fusion.2) | copy-start | bytes 6291460
  477.5 106.1 %all-reduce.27.cloned.1.call-start = ((), (), s32[]{:S(2)}) async-start(), calls=%async_computation.8 | async-start | bytes 262144 | tf_op jit(solution)/shard_map/psum | solution.py:50
  539.3 2.9 copy-start.8
  544.6 2.4 copy-start.6
  549.5 72.0 %all-reduce.23.cloned.1.call-start = ((), (), s32[]{:S(2)}) async-start(), calls=%async_computation.6 | async-start | bytes 393216 | tf_op jit(solution)/shard_map/psum | solution.py:50
  564.0 236.7 %all-reduce.25.cloned.1.call-start = ((), (), s32[]{:S(2)}) async-start(), calls=%async_computation.7 | async-start | bytes 4194304 | tf_op jit(solution)/shard_map/psum | solution.py:65
  602.2 2.2 copy-start.9
  604.4 19.7 %copy-start.22 = (f32[64,64]{1,0:T(8,128)S(1)}, f32[64,64]{1,0:T(8,128)}, u32[]{:S(2)}) copy-start(f32[64,64]{1,0:T(8,128)} %get-tuple-element.10) | copy-start | bytes 49156
  604.4 19.7 %copy-start.23 = (f32[64,64]{1,0:T(8,128)S(1)}, f32[64,64]{1,0:T(8,128)}, u32[]{:S(2)}) copy-start(f32[64,64]{1,0:T(8,128)} %get-tuple-element.11) | copy-start | bytes 49156
  606.5 26.5 %copy-start.10 = (f32[8192,64]{0,1:T(8,128)}, f32[8192,64]{0,1:T(8,128)S(1)}, u32[]{:S(2)}) copy-start(f32[8192,64]{0,1:T(8,128)S(1)} %convolution_subtract_fusion) | copy-start | bytes 6291460
  632.9 8.6 %copy-start.14 = (f32[64,8192]{1,0:T(8,128)S(1)}, f32[64,8192]{1,0:T(8,128)}, u32[]{:S(2)}) copy-start(f32[64,8192]{1,0:T(8,128)} %fusion.12) | copy-start | bytes 6291460
  739.9 5.0 copy-start.15
  744.9 3.3 copy-start.11
  840.4 4.1 copy-start.18
  842.4 2.2 copy-start.17
  (7 other events, 11.6 us)
Sparse Core Ops, SparseCore 0:
  9.5 13.2 all-gather.2
  24.4 25.8 all-gather.4
  61.6 36.1 all-reduce.14
  216.3 61.1 all-reduce.16
  287.4 33.9 all-reduce.28
  324.2 34.8 all-reduce.18
  477.6 61.6 all-reduce.20
  549.6 33.9 all-reduce.26
  586.5 34.9 all-reduce.22
  739.3 61.3 all-reduce.24
where the time goes:
time: 862 us; the launch traced here: 853 us
  matrix products  328 us (38%)
  waiting for transfers between devices  310 us (36%)
  blocking collectives  147 us (17%)
  other arithmetic  47.9 us (6%)
  between operations  15.6 us (2%)
    psum x3, waiting for transfers between devices, shards(): summed = lax.psum(feature_term, ('samples', 'rhs'))  165 us
    psum x3, blocking collectives, shards(): lax.psum(apply_partial_value, 'features').astype(jnp.bfloat16)  127 us
    psum x5, waiting for transfers between devices, totals(): return lax.psum(values, 'features')  105 us
    dot_general x3, matrix products, shards(): jnp.dot(design, narrow, preferred_element_type=jnp.float32)  85.3 us
    dot_general x3, matrix products, shards(): lax.dot_general(design, narrow_images, (((0,), (0,)), ((), ())), preferre...  77.8 us
    dot_general x12, matrix products, inner_prod(): lax.dot_general(left, right, (((0,), (0,)), ((), ())), precision=lax.Prec...  30.3 us
    dot_general x3, matrix products, factor_times(): second = jnp.dot(factor_narrow, lower, preferred_element_type=jnp.float32)  27.1 us
    all_gather x1, waiting for transfers between devices, shards(): basis_rows = lax.all_gather(factor, 'rhs', axis=1, tiled=True)  25.6 us
  transfers between devices with their start and end apart: 10, of which 10 were waited for; matrix products, arithmetic and copies ran while one was open for 11% of the time, Pallas kernels for 0%

commit v1 on v0

--- a/solution.py
+++ b/solution.py
@@ -62,7 +62,7 @@
         feature_term = lax.dot_general(
             design, narrow_images, (((0,), (0,)), ((), ())), preferred_element_type=jnp.float32
         )
-        summed = lax.psum(feature_term, ("samples", "rhs"))
+        summed = jnp.sum(lax.all_gather(feature_term, ("samples", "rhs")), 0)
         applied = summed + ridge_weight * direction
         gram_block, cross_term, image_res, image_image, factor_image = totals(
             (

time: 862 us -> 1020 us (1.18)
  waiting for transfers between devices: 310 us -> 397 us
  local copies, waits for them, and re-layouts: 4.31 us -> 52.8 us
  blocking collectives: 147 us -> 159 us
  other arithmetic: 47.9 us -> 58.9 us
    all_gather x0 -> x3, waiting for transfers between devices: none -> 249 us  [shards(): summed = jnp.sum(lax.all_gather(feature_term, ('samples', 'rhs')), 0)]
    psum x3 -> x0, waiting for transfers between devices: 165 us -> none  [shards(): summed = lax.psum(feature_term, ('samples', 'rhs'))]
    unnamed x58 -> x65, local copies, waits for them, and re-layouts: 2.36 us -> 50.8 us
    reduce_sum x0 -> x3, other arithmetic: none -> 15.6 us  [shards(): summed = jnp.sum(lax.all_gather(feature_term, ('samples', 'rhs')), 0)]
    psum x3, blocking collectives: 127 us -> 139 us  [shards(): lax.psum(apply_partial_value, 'features').astype(jnp.bfloat16)]
  transfers between devices with their start and end apart: 10 -> 10, of which waited for: 10 -> 10; matrix products, arithmetic and copies ran while one was open for 11% -> 9% of each run, Pallas kernels for 0% -> 0%
where the time goes in v1:
time: 1020 us; the launch traced here: 1010 us
  waiting for transfers between devices  397 us (39%)
  matrix products  324 us (32%)
  blocking collectives  159 us (16%)
  other arithmetic  58.9 us (6%)
  local copies, waits for them, and re-layouts  52.8 us (5%)
  between operations  16 us (2%)
    all_gather x3, waiting for transfers between devices, shards(): summed = jnp.sum(lax.all_gather(feature_term, ('samples', 'rhs')), 0)  249 us
    psum x3, blocking collectives, shards(): lax.psum(apply_partial_value, 'features').astype(jnp.bfloat16)  139 us
    psum x5, waiting for transfers between devices, totals(): return lax.psum(values, 'features')  107 us
    dot_general x3, matrix products, shards(): jnp.dot(design, narrow, preferred_element_type=jnp.float32)  85.3 us
    dot_general x3, matrix products, shards(): lax.dot_general(design, narrow_images, (((0,), (0,)), ((), ())), preferre...  77.8 us
    unnamed x65, local copies, waits for them, and re-layouts  50.8 us
    dot_general x12, matrix products, inner_prod(): lax.dot_general(left, right, (((0,), (0,)), ((), ())), precision=lax.Prec...  28.7 us
    dot_general x3, matrix products, factor_times(): second = jnp.dot(factor_narrow, lower, preferred_element_type=jnp.float32)  27.1 us
  transfers between devices with their start and end apart: 10, of which 10 were waited for; matrix products, arithmetic and copies ran while one was open for 9% of the time, Pallas kernels for 0%

profile of v1, /device:TPU:0, one launch (start us, length us, event | category | flops | bytes accessed | tf_op | source)
XLA Modules:
  0.0 1009.1 jit_solution(7697882092860864411)
XLA Ops:
  10.0 12.9 %all-gather.9.cloned.1.call-done = f32[8192,64]{0,1:T(8,128)} async-done(((f32[8192,32]{0,1:T(8,128)}), f32[8192,64]{0,1:T(8,128)}) %all-gather.9.cloned.1.call-update) | async-done | bytes 2097168 | tf_op jit(solution)/shard_map/all_gather | solution.py:45
  24.7 25.6 %all-gather.11.cloned.1.call-done = bf16[8192,768]{1,0:T(8,128)(2,1)} async-done(((bf16[8192,384]{1,0:T(8,128)(2,1)}), bf16[8192,768]{1,0:T(8,128)(2,1)}) %all-gather.11.cloned.1.call-update) | async-done | bytes 12582928 | tf_op jit(solution)/shard_map/all_gather | solution.py:47
  50.3 7.0 convolution_bitcast_fusion.6
  61.5 36.3 %all-reduce.12.cloned.1.call-done = f32[768,64]{0,1:T(8,128)} async-done(((f32[768,64]{0,1:T(8,128)}), f32[768,64]{0,1:T(8,128)}) %all-reduce.12.cloned.1.call-update) | async-done | bytes 196624 | tf_op jit(solution)/shard_map/psum | solution.py:50
  98.7 8.5 fusion.67
  107.2 9.8 fusion.3
  117.1 30.4 %convolution_bitcast_fusion.5 = f32[4096,64]{0,1:T(8,128)S(1)} fusion(bf16[4096,8192]{1,0:T(8,128)(2,1)} %param.11, f32[8192,64]{0,1:T(8,128)} %fusion.3), kind=kOutput, calls=%fused_computation.21 | convolution fusion | flops 4295491584 | bytes 70254592 | tf_op jit(solution)/shard_map/dot_general | solution.py:60
  147.5 55.1 %all-reduce.21 = bf16[4096,64]{0,1:T(8,128)(2,1)} all-reduce(f32[4096,64]{0,1:T(8,128)S(1)} %convolution_bitcast_fusion.5), channel_id=1, replica_groups=mesh['samples'=4,'features'=4,'rhs'=2] {'features'}, use_global_device_ids=true, to_apply=%region_2.0 | all-reduce | flops 262144 | bytes 1572864 | tf_op jit(solution)/shard_map/psum | solution.py:61
  202.6 25.9 %convolution_bitcast_fusion.2 = f32[8192,64]{0,1:T(8,128)} fusion(bf16[4096,8192]{1,0:T(8,128)(2,1)} %param.11, bf16[4096,64]{0,1:T(8,128)(2,1)} %all-reduce.21), kind=kOutput, calls=%fused_computation.13 | convolution fusion | flops 4294967296 | bytes 69730304 | tf_op jit(solution)/shard_map/dot_general | solution.py:62
  232.6 85.4 %all-gather.13.cloned.1.call-done = f32[65536,64]{0,1:T(8,128)} async-done(((f32[8192,64]{0,1:T(8,128)}), f32[65536,64]{0,1:T(8,128)}) %all-gather.13.cloned.1.call-update) | async-done | bytes 16777232 | tf_op jit(solution)/shard_map/all_gather | solution.py:65
  317.9 15.2 %copy.12 = f32[8,8,8,8192]{3,2,1,0:T(8,128)S(1)} copy(f32[8,8,8,8192]{3,1,2,0:T(8,128)} %bitcast.223) | data formatting | bytes 33554432
  352.8 7.6 fusion.22
  360.9 20.1 %all-reduce.20.cloned.1.call-done = (f32[64,64]{1,0:T(8,128)}, f32[64,64]{1,0:T(8,128)}, f32[64,64]{1,0:T(8,128)}, f32[64,64]{1,0:T(8,128)}) async-done(((f32[64,64]{1,0:T(8,128)}, f32[64,64]{1,0:T(8,128)}, f32[64,64]{1,0:T(8,128)}, f32[64,64]{1,0:T(8,128)}), (f32[64,64]{1,0:T(8,128)}, f32[64,64]{1,0:T(8,128)}, f32[64,64]{1,0:T(8,128)}, f32[64,64]{1,0:T(8,128)})) %all-reduce.20.cloned.1.call-update) | async-done | bytes 65552 | tf_op jit(solution)/shard_map/psum | solution.py:50
  402.5 16.1 %all-reduce.14.cloned.1.call-done = f32[768,64]{0,1:T(8,128)} async-done(((f32[768,64]{0,1:T(8,128)}), f32[768,64]{0,1:T(8,128)}) %all-reduce.14.cloned.1.call-update) | async-done | bytes 196624 | tf_op jit(solution)/shard_map/psum | solution.py:50
  421.6 8.4 fusion.72
  430.1 8.6 fusion.4
  441.0 27.8 %convolution_bitcast_fusion.4 = f32[4096,64]{0,1:T(8,128)S(1)} fusion(bf16[4096,8192]{1,0:T(8,128)(2,1)} %param.11, f32[8192,64]{0,1:T(8,128)S(1)} %convolution_add_fusion.2), kind=kOutput, calls=%fused_computation.20 | convolution fusion | flops 4295491584 | bytes 70254592 | tf_op jit(solution)/shard_map/dot_general | solution.py:60
  468.9 42.1 %all-reduce.22 = bf16[4096,64]{0,1:T(8,128)(2,1)} all-reduce(f32[4096,64]{0,1:T(8,128)S(1)} %convolution_bitcast_fusion.4), channel_id=1, replica_groups=mesh['samples'=4,'features'=4,'rhs'=2] {'features'}, use_global_device_ids=true, to_apply=%region_11.0 | all-reduce | flops 262144 | bytes 1572864 | tf_op jit(solution)/shard_map/psum | solution.py:61
  511.0 25.9 %convolution_bitcast_fusion.1 = f32[8192,64]{0,1:T(8,128)} fusion(bf16[4096,8192]{1,0:T(8,128)(2,1)} %param.11, bf16[4096,64]{0,1:T(8,128)(2,1)} %all-reduce.22), kind=kOutput, calls=%fused_computation.8 | convolution fusion | flops 4294967296 | bytes 69730304 | tf_op jit(solution)/shard_map/dot_general | solution.py:62
  541.0 85.4 %all-gather.15.cloned.1.call-done = f32[65536,64]{0,1:T(8,128)} async-done(((f32[8192,64]{0,1:T(8,128)}), f32[65536,64]{0,1:T(8,128)}) %all-gather.15.cloned.1.call-update) | async-done | bytes 16777232 | tf_op jit(solution)/shard_map/all_gather | solution.py:65
  626.4 15.4 %copy.13 = f32[8,8,8,8192]{3,2,1,0:T(8,128)S(1)} copy(f32[8,8,8,8192]{3,1,2,0:T(8,128)} %bitcast.224) | data formatting | bytes 33554432
  662.8 7.6 fusion.23
  670.9 20.0 %all-reduce.18.cloned.1.call-done = (f32[64,64]{1,0:T(8,128)}, f32[64,64]{1,0:T(8,128)}, f32[64,64]{1,0:T(8,128)}, f32[64,64]{1,0:T(8,128)}) async-done(((f32[64,64]{1,0:T(8,128)}, f32[64,64]{1,0:T(8,128)}, f32[64,64]{1,0:T(8,128)}, f32[64,64]{1,0:T(8,128)}), (f32[64,64]{1,0:T(8,128)}, f32[64,64]{1,0:T(8,128)}, f32[64,64]{1,0:T(8,128)}, f32[64,64]{1,0:T(8,128)})) %all-reduce.18.cloned.1.call-update) | async-done | bytes 65552 | tf_op jit(solution)/shard_map/psum | solution.py:50
  714.1 14.8 %all-reduce.16.cloned.1.call-done = f32[768,64]{0,1:T(8,128)} async-done(((f32[768,64]{0,1:T(8,128)}), f32[768,64]{0,1:T(8,128)}) %all-reduce.16.cloned.1.call-update) | async-done | bytes 196624 | tf_op jit(solution)/shard_map/psum | solution.py:50
  731.8 8.4 fusion.79
  740.3 8.6 fusion.5
  751.1 27.1 %convolution_bitcast_fusion.3 = f32[4096,64]{0,1:T(8,128)S(1)} fusion(bf16[4096,8192]{1,0:T(8,128)(2,1)} %param.11, f32[8192,64]{0,1:T(8,128)S(1)} %convolution_add_fusion), kind=kOutput, calls=%fused_computation.19 | convolution fusion | flops 4295491584 | bytes 70254592 | tf_op jit(solution)/shard_map/dot_general | solution.py:60
  778.2 42.1 %all-reduce.23 = bf16[4096,64]{0,1:T(8,128)(2,1)} all-reduce(f32[4096,64]{0,1:T(8,128)S(1)} %convolution_bitcast_fusion.3), channel_id=1, replica_groups=mesh['samples'=4,'features'=4,'rhs'=2] {'features'}, use_global_device_ids=true, to_apply=%region_18.0 | all-reduce | flops 262144 | bytes 1572864 | tf_op jit(solution)/shard_map/psum | solution.py:61
  820.3 26.0 %convolution_bitcast_fusion = f32[8192,64]{0,1:T(8,128)} fusion(bf16[4096,8192]{1,0:T(8,128)(2,1)} %param.11, bf16[4096,64]{0,1:T(8,128)(2,1)} %all-reduce.23), kind=kOutput, calls=%fused_computation.3 | convolution fusion | flops 4294967296 | bytes 69730304 | tf_op jit(solution)/shard_map/dot_general | solution.py:62
  857.2 78.6 %all-gather.17.cloned.1.call-done = f32[65536,64]{0,1:T(8,128)} async-done(((f32[8192,64]{0,1:T(8,128)}), f32[65536,64]{0,1:T(8,128)}) %all-gather.17.cloned.1.call-update) | async-done | bytes 16777232 | tf_op jit(solution)/shard_map/all_gather | solution.py:65
  935.7 15.4 %copy.14 = f32[8,8,8,8192]{3,2,1,0:T(8,128)S(1)} copy(f32[8,8,8,8192]{3,1,2,0:T(8,128)} %bitcast.222) | data formatting | bytes 33554432
  959.6 19.9 %all-reduce = (f32[64,64]{1,0:T(8,128)S(1)}, f32[64,64]{1,0:T(8,128)S(1)}) all-reduce(f32[64,64]{1,0:T(8,128)S(1)} %fusion.19, f32[64,64]{1,0:T(8,128)S(1)} %fusion.83), channel_id=1, replica_groups=mesh['samples'=4,'features'=4,'rhs'=2] {'features'}, use_global_device_ids=true, to_apply=%region_20.25 | all-reduce | flops 8192 | bytes 65536 | tf_op jit(solution)/shard_map/psum | solution.py:50
  (159 shorter events, 155.0 us)
Async XLA Ops:
  7.2 15.7 %all-gather.9.cloned.1.call-start = ((), (), s32[]{:S(2)}) async-start(), calls=%async_computation | async-start | bytes 3145728 | tf_op jit(solution)/shard_map/all_gather | solution.py:45
  7.9 42.4 %all-gather.11.cloned.1.call-start = ((), (), s32[]{:S(2)}) async-start(), calls=%async_computation.1 | async-start | bytes 18874368 | tf_op jit(solution)/shard_map/all_gather | solution.py:47
  8.7 89.1 %all-reduce.12.cloned.1.call-start = ((), (), s32[]{:S(2)}) async-start(), calls=%async_computation.2 | async-start | bytes 393216 | tf_op jit(solution)/shard_map/psum | solution.py:50
  22.8 27.4 %copy-start.1 = (f32[8192,64]{0,1:T(8,128)S(1)}, f32[8192,64]{0,1:T(8,128)}, u32[]{:S(2)}) copy-start(f32[8192,64]{0,1:T(8,128)} %all-gather.9.cloned.1.call-done) | copy-start | bytes 6291460
  50.3 8.2 copy-start
  61.5 256.5 %all-gather.13.cloned.1.call-start = ((), (), s32[]{:S(2)}) async-start(), calls=%async_computation.5 | async-start | bytes 18874368 | tf_op jit(solution)/shard_map/all_gather | solution.py:65
  98.7 8.5 copy-start.21
  228.5 152.5 %all-reduce.20.cloned.1.call-start = ((), (), s32[]{:S(2)}) async-start(), calls=%async_computation.9 | async-start | bytes 262144 | tf_op jit(solution)/shard_map/psum | solution.py:50
  333.2 5.2 copy-start.4
  341.1 2.4 copy-start.2
  345.9 72.7 %all-reduce.14.cloned.1.call-start = ((), (), s32[]{:S(2)}) async-start(), calls=%async_computation.3 | async-start | bytes 393216 | tf_op jit(solution)/shard_map/psum | solution.py:50
  360.4 265.9 %all-gather.15.cloned.1.call-start = ((), (), s32[]{:S(2)}) async-start(), calls=%async_computation.6 | async-start | bytes 18874368 | tf_op jit(solution)/shard_map/all_gather | solution.py:65
  396.7 3.3 copy-start.28
  396.7 3.5 copy-start.3
  400.2 21.0 %copy-start.26 = (f32[64,64]{1,0:T(8,128)S(1)}, f32[64,64]{1,0:T(8,128)}, u32[]{:S(2)}) copy-start(f32[64,64]{1,0:T(8,128)} %get-tuple-element.14) | copy-start | bytes 49156
  400.2 21.0 %copy-start.27 = (f32[64,64]{1,0:T(8,128)S(1)}, f32[64,64]{1,0:T(8,128)}, u32[]{:S(2)}) copy-start(f32[64,64]{1,0:T(8,128)} %get-tuple-element.15) | copy-start | bytes 49156
  402.3 27.8 %copy-start.8 = (f32[8192,64]{0,1:T(8,128)}, f32[8192,64]{0,1:T(8,128)S(1)}, u32[]{:S(2)}) copy-start(f32[8192,64]{0,1:T(8,128)S(1)} %convolution_subtract_fusion.1) | copy-start | bytes 6291460
  430.1 8.7 copy-start.16
  441.0 96.0 %copy-start.6 = (f32[8192,64]{0,1:T(8,128)}, f32[8192,64]{0,1:T(8,128)S(1)}, u32[]{:S(2)}) copy-start(f32[8192,64]{0,1:T(8,128)S(1)} %convolution_add_fusion.2) | copy-start | bytes 6291460
  536.9 154.0 %all-reduce.18.cloned.1.call-start = ((), (), s32[]{:S(2)}) async-start(), calls=%async_computation.8 | async-start | bytes 262144 | tf_op jit(solution)/shard_map/psum | solution.py:50
  641.8 5.2 copy-start.7
  655.9 73.0 %all-reduce.16.cloned.1.call-start = ((), (), s32[]{:S(2)}) async-start(), calls=%async_computation.4 | async-start | bytes 393216 | tf_op jit(solution)/shard_map/psum | solution.py:50
  670.4 265.4 %all-gather.17.cloned.1.call-start = ((), (), s32[]{:S(2)}) async-start(), calls=%async_computation.7 | async-start | bytes 18874368 | tf_op jit(solution)/shard_map/all_gather | solution.py:65
  709.6 2.2 copy-start.10
  711.8 19.6 %copy-start.24 = (f32[64,64]{1,0:T(8,128)S(1)}, f32[64,64]{1,0:T(8,128)}, u32[]{:S(2)}) copy-start(f32[64,64]{1,0:T(8,128)} %get-tuple-element.10) | copy-start | bytes 49156
  711.8 19.6 %copy-start.25 = (f32[64,64]{1,0:T(8,128)S(1)}, f32[64,64]{1,0:T(8,128)}, u32[]{:S(2)}) copy-start(f32[64,64]{1,0:T(8,128)} %get-tuple-element.11) | copy-start | bytes 49156
  713.9 26.4 %copy-start.11 = (f32[8192,64]{0,1:T(8,128)}, f32[8192,64]{0,1:T(8,128)S(1)}, u32[]{:S(2)}) copy-start(f32[8192,64]{0,1:T(8,128)S(1)} %convolution_subtract_fusion) | copy-start | bytes 6291460
  740.3 8.6 copy-start.17
  847.1 5.0 copy-start.18
  852.0 3.3 copy-start.12
  996.0 4.1 copy-start.20
  998.0 2.2 copy-start.19
  (9 other events, 14.4 us)
Sparse Core Ops, SparseCore 0:
  9.5 13.2 all-gather.8
  24.4 25.8 all-gather.10
  61.6 36.1 all-reduce.11
  228.6 89.2 all-gather.12
  346.1 34.8 all-reduce.19
  383.7 34.8 all-reduce.13
  537.1 89.2 all-gather.14
  656.0 34.9 all-reduce.17
  693.9 34.9 all-reduce.15
  846.4 89.2 all-gather.16
